TPU v7x, 32 devices: a whole 2x2x4 slice. The times are simulated.
32 devices in a mesh: blk: 8 (over y, x, core), lvl: 4 (over z).
Axes of the slice: x: 2, y: 2, z: 4, core: 2. Of those that a mesh axis runs over, the one named last changes fastest.
Arguments:
- vorticity: bfloat16 [4, 3, 64, 32768], P('lvl', None, 'blk'), may hold values from -6 to 6
- shift_field: bfloat16 [4, 64, 32768], P('lvl', 'blk'), may hold values from -0.8984375 to 0.8984375
- new_index: int32 [4, 64], P('lvl', 'blk'), may hold values from 0 to 63, as said below
- parent_slot: int32 [4, 64], P('lvl', 'blk'), may hold values from 0 to 511, as said below
- flags: int32 [4, 64], P('lvl', 'blk'), may hold values 0 or 1
Outputs:
- field: bfloat16 [4, 3, 64, 32768], P('lvl', None, 'blk')
Inputs may be any that keep to these rules, and one draw needn't show every extreme that they name: `new_index`: in each level a permutation of the block positions; position b lies on device b // 8 of blk. No device sends more than 2 of its blocks to one device, and that number is reached. `parent_slot`: in each level all values differ; value // 8 is a block of the next coarser level and lies on device value // 64. No device has more than 2 blocks whose parents lie on one device, counting the blocks it holds before migration or those it holds after, and that number is reached in both. The values of level 0 are not used.
All inputs are finite; a program needn't handle non-finite values. No bound on the sum of `flags` on one device may be relied on, other than what follows from the above.
Results may differ from a plain program's by a relative error of at most 0.001.
Values may be sent and summed in bfloat16 or wider, within the bound.
A program may use at most 128 MiB of HBM per device.

v0:
```python
import functools

import jax
import jax.numpy as jnp
import numpy as np
from jax import lax
from jax.experimental import pallas as pl
from jax.experimental.pallas import tpu as pltpu
from jax.sharding import PartitionSpec as P

MESH = pl.DeviceIdType.MESH
EDGE = 32
PLANE = EDGE * EDGE
LANE_TILES = PLANE // 128
CAP = 2
SPAN = 8
ORDER = (1, 2, 0, 3)
VMEM_LIMIT = 60 * 1024 * 1024
PIECES = ((4 * PLANE, 20 * PLANE), (20 * PLANE, 32 * PLANE), (0, 4 * PLANE))


def device(blk, lvl):
    return {"blk": blk, "lvl": lvl}


def remote(src, dst, send, recv, target):
    return pltpu.make_async_remote_copy(
        src_ref=src, dst_ref=dst, send_sem=send, recv_sem=recv, device_id=target, device_id_type=MESH
    )


def tap_weights(shifts):
    size = jnp.abs(shifts)
    rest = 1.0 - size
    size2 = size * size
    rest2 = rest * rest
    middle = 1.0 + size2 * (1.5 * size - 2.5)
    ahead = 1.0 + rest2 * (1.5 * rest - 2.5)
    behind = -0.5 * rest2 * size
    far = -0.5 * size2 * rest
    up = shifts >= 0.0
    return {
        -2: jnp.where(up, 0.0, far),
        -1: jnp.where(up, behind, ahead),
        0: middle,
        1: jnp.where(up, ahead, behind),
        2: jnp.where(up, far, 0.0),
    }


def split(value, size):
    if size & (size - 1) == 0:
        return lax.shift_right_logical(value, size.bit_length() - 1), lax.bitwise_and(value, size - 1)
    return lax.div(value, size), lax.rem(value, size)


def picks(keys, wanted):
    count, first, second = jnp.int32(0), jnp.int32(0), jnp.int32(0)
    for b, key in enumerate(keys):
        hit = key == wanted
        first = jnp.where(jnp.logical_and(hit, count == 0), b, first)
        second = jnp.where(jnp.logical_and(hit, count == 1), b, second)
        count = count + hit.astype(jnp.int32)
    return first, second


def kernel(n, levels, spots_in, parents_in, flags_in, vort_in, shift_in, shrink_in, grow_in, out,
           spots, parent_slot, flags, field, shrink, grow,
           rows, patch, whole, masks, result,
           send0, send1, send2, send3, got0, got1, got2, got3,
           small, ghost, got_ghost,
           edge, edge_low, edge_high, below, above, halo_low, halo_high,
           tab, near_tabs, fine_tabs, near_local, fine_local, line, place, line2, octants,
           pick, pick_ghost,
           in_sem, index_sem, table_sem, halo_s, halo_r, near_s, near_r, coarse_s, coarse_r,
           block_s, block_r, ghost_s, ghost_r, out_sem, ready):
    me = lax.axis_index("blk")
    lvl = lax.axis_index("lvl")
    blocks = out.shape[1]
    spread = EDGE * LANE_TILES * blocks
    piece = SPAN * LANE_TILES
    coarse_level = jnp.maximum(lvl - 1, 0)
    fine_level = jnp.minimum(lvl + 1, levels - 1)
    sends, gots = (send0, send1, send2, send3), (got0, got1, got2, got3)
    after = device(lax.rem(me + 1, n), lvl)
    before = device(lax.rem(me + n - 1, n), lvl)
    has_coarse, has_fine = lvl > 0, lvl < levels - 1
    not_first, not_last = me > 0, me < n - 1

    barrier = pltpu.get_barrier_semaphore()

    def greet(blk, level):
        pl.semaphore_signal(barrier, inc=1, device_id=device(blk, level), device_id_type=MESH)

    for k in range(1, n):
        greet(lax.rem(me + k, n), lvl)

    @pl.when(has_coarse)
    def _():
        greet(me, coarse_level)

    @pl.when(has_fine)
    def _():
        greet(me, fine_level)

    index_loads = [
        pltpu.make_async_copy(src, dst, index_sem.at[i])
        for i, (src, dst) in enumerate(((spots_in, spots), (parents_in, parent_slot), (flags_in, flags)))
    ]
    loads = []
    for i, (lo, hi) in enumerate(PIECES):
        part = pl.ds(lo, hi - lo)
        loads.append((
            pltpu.make_async_copy(shift_in.at[:, part], field.at[3, :, part], in_sem.at[2 * i]),
            pltpu.make_async_copy(vort_in.at[:, :, part], field.at[pl.ds(0, 3), :, part], in_sem.at[2 * i + 1]),
        ))
    constants = (
        pltpu.make_async_copy(shrink_in, shrink, table_sem.at[0]),
        pltpu.make_async_copy(grow_in, grow, table_sem.at[1]),
    )
    for copy in index_loads:
        copy.start()
    for pair in loads:
        for copy in pair:
            copy.start()
    for copy in constants:
        copy.start()

    sublane = lax.broadcasted_iota(jnp.int32, (blocks, 128), 0)
    lane = lax.broadcasted_iota(jnp.int32, (1, 128), 1)

    def tile(f, x, j):
        at = pl.multiple_of(x * PLANE + j * 128, 128)
        return field[f, :, pl.ds(at, 128)].astype(jnp.float32)

    def source_tile(f, x, j):
        if x < 0:
            edge_row = halo_low[pl.ds(f * 16 + (x + 2) * LANE_TILES + j, 1), :]
            return jnp.where(sublane == 0, edge_row, pltpu.roll(tile(f, x + EDGE, j), 1, 0))
        if x >= EDGE:
            edge_row = halo_high[pl.ds(f * 16 + (x - EDGE) * LANE_TILES + j, 1), :]
            return jnp.where(sublane == blocks - 1, edge_row, pltpu.roll(tile(f, x - EDGE, j), blocks - 1, 0))
        return tile(f, x, j)

    def remesh(part):
        x0, x1 = part * SPAN, (part + 1) * SPAN

        def chunk(j, carry):
            sums = [{}, {}, {}]
            for x in range(x0 - 2, x1 + 2):
                weights = tap_weights(source_tile(3, x, j))
                for c in range(3):
                    value = source_tile(c, x, j)
                    for offset in range(-2, 3):
                        to = x + offset
                        if x0 <= to < x1:
                            term = value * weights[offset]
                            sums[c][to] = sums[c][to] + term if to in sums[c] else term
                    if x0 <= x - 2:
                        at = c * spread + ((x - 2) * LANE_TILES + j) * blocks
                        rows[pl.ds(pl.multiple_of(at, blocks), blocks), :] = sums[c].pop(x - 2)
            return carry

        lax.fori_loop(0, LANE_TILES, chunk, 0)
        for b in range(blocks):
            for c in range(3):
                at = c * spread + x0 * LANE_TILES * blocks + b
                whole[part, b, c * piece:(c + 1) * piece, :] = rows[
                    pl.ds(at, piece, stride=blocks), :
                ].astype(jnp.bfloat16)

    def pack(part):
        def one(k, carry):
            to = lax.rem(me + k, n)
            for s in range(CAP):
                sends[part][to, s] = whole[part, pick[CAP * to + s]]
            return carry

        lax.fori_loop(1, n, one, 0)

    def keep(part):
        for s in range(CAP):
            gots[part][CAP * me + s] = whole[part, pick[CAP * me + s]]

    def block_copy(part, k):
        to = lax.rem(me + k, n)
        return remote(sends[part].at[to], gots[part].at[pl.ds(CAP * me, CAP)],
                      block_s.at[part, k], block_r.at[part, k], device(to, lvl))

    def block_arrival(part, k):
        source = lax.rem(me + n - k, n)
        return remote(sends[part].at[me], gots[part].at[pl.ds(CAP * source, CAP)],
                      block_s.at[part, k], block_r.at[part, k], before)

    def send_blocks(part):
        for k in range(1, n):
            block_copy(part, k).start()

    def near(k):
        return remote(tab, near_tabs.at[me], near_s.at[k], near_r.at[k], device(lax.rem(me + k, n), lvl))

    def near_arrival(k):
        return remote(tab, near_tabs.at[lax.rem(me + n - k, n)], near_s.at[k], near_r.at[k], before)

    def coarse(k):
        return remote(tab, fine_tabs.at[me], coarse_s.at[k], coarse_r.at[k],
                      device(lax.rem(me + k, n), coarse_level))

    def coarse_arrival(k):
        return remote(tab, fine_tabs.at[lax.rem(me + n - k, n)], coarse_s.at[k], coarse_r.at[k], before)

    def ghost_copy(k):
        to = lax.rem(me + k, n)
        return remote(ghost.at[to], got_ghost.at[pl.ds(CAP * me, CAP)], ghost_s.at[k], ghost_r.at[k],
                      device(to, coarse_level))

    def ghost_arrival(k):
        source = lax.rem(me + n - k, n)
        return remote(ghost.at[me], got_ghost.at[pl.ds(CAP * source, CAP)], ghost_s.at[k], ghost_r.at[k], before)

    def high(target):
        return remote(edge_high, below, halo_s.at[0], halo_r.at[0], target)

    def low(target):
        return remote(edge_low, above, halo_s.at[1], halo_r.at[1], target)

    for copy in index_loads:
        copy.wait()
    head = jnp.zeros((1, 128), jnp.int32)
    for part, ref in enumerate((spots, parent_slot, flags)):
        for b in range(blocks):
            head = jnp.where(lane == part * blocks + b, ref[0, b], head)
    tab[...] = head
    near_tabs[me] = head
    owners = [split(spots[0, b], blocks)[0] for b in range(blocks)]

    def choose(to, carry):
        first, second = picks(owners, to)
        pick[CAP * to] = first
        pick[CAP * to + 1] = second
        return carry

    lax.fori_loop(0, n, choose, 0)

    for copy in loads[0]:
        copy.wait()
    remesh(ORDER[0])
    pack(ORDER[0])
    for copy in loads[1] + loads[2]:
        copy.wait()

    def edges(j, carry):
        for f in range(4):
            for p in range(2):
                at = f * 16 + p * LANE_TILES + j
                edge[pl.ds(at, 1), :] = tile(f, p, j)[0:1, :]
                edge[pl.ds(64 + at, 1), :] = tile(f, EDGE - 2 + p, j)[blocks - 1:blocks, :]
        return carry

    lax.fori_loop(0, LANE_TILES, edges, 0)
    edge_low[...] = edge[0:64, :].astype(jnp.bfloat16)
    edge_high[...] = edge[64:128, :].astype(jnp.bfloat16)

    nearby = n - 1 + has_coarse.astype(jnp.int32) + has_fine.astype(jnp.int32)
    pl.semaphore_wait(barrier, nearby)

    @pl.when(not_last)
    def _():
        high(after).start()

    @pl.when(not_first)
    def _():
        low(before).start()

    for k in range(1, n):
        near(k).start()
    send_blocks(ORDER[0])

    @pl.when(has_fine)
    def _():
        pl.semaphore_signal(ready, inc=1, device_id=device(me, fine_level), device_id_type=MESH)

    keep(ORDER[0])
    remesh(ORDER[1])
    pack(ORDER[1])
    send_blocks(ORDER[1])
    keep(ORDER[1])

    @pl.when(not_last)
    def _():
        low(after).wait_recv()

    @pl.when(not_first)
    def _():
        high(before).wait_recv()

    halo_low[...] = jnp.where(not_first, below[...].astype(jnp.float32), 0.0)
    halo_high[...] = jnp.where(not_last, above[...].astype(jnp.float32), 0.0)
    for part in ORDER[2:]:
        remesh(part)
        pack(part)
        send_blocks(part)
        keep(part)

    @pl.when(has_coarse)
    def _():
        pl.semaphore_wait(ready, 1)
        for k in range(n):
            coarse(k).start()

    for k in range(1, n):
        near_arrival(k).wait_recv()
    fetch_near = pltpu.make_async_copy(near_tabs, near_local, table_sem.at[2])
    fetch_near.start()
    fetch_near.wait()
    for copy in constants:
        copy.wait()

    @pl.when(has_coarse)
    def _():
        parents = []
        for b in range(blocks):
            home, spot = split(spots[0, b], blocks)
            parents.append(split(near_local[home, 0, blocks + spot], 8 * blocks)[0])

        def choose_ghost(to, carry):
            first, second = picks(parents, to)
            pick_ghost[CAP * to] = first
            pick_ghost[CAP * to + 1] = second
            return carry

        lax.fori_loop(0, n, choose_ghost, 0)

        def restrict(b, carry):
            columns = []
            for half in range(2):
                for dx in range(2):
                    for odd in range(2):
                        parts = []
                        for c in range(3):
                            for jj in range(4):
                                x, j = half * 16 + dx, 2 * jj + odd
                                at = c * spread + (x * LANE_TILES + j) * blocks + b
                                parts.append(rows[pl.ds(at, 8, stride=2 * LANE_TILES * blocks), :])
                        columns.append(jnp.concatenate(parts, axis=0).astype(jnp.bfloat16))
            wide = jnp.concatenate(columns, axis=1)
            small[b] = jnp.dot(wide, shrink[...], preferred_element_type=jnp.float32).astype(jnp.bfloat16)
            return carry

        lax.fori_loop(0, blocks, restrict, 0)

        def pack_ghost(to, carry):
            for s in range(CAP):
                ghost[to, s] = small[pick_ghost[CAP * to + s]]
            return carry

        lax.fori_loop(0, n, pack_ghost, 0)
        for k in range(n):
            ghost_copy(k).start()

    def settle_places(source, places):
        count = jnp.int32(0)
        for b in range(blocks):
            owner, spot = split(near_local[source, 0, b], blocks)
            mine = owner == me
            slot = CAP * source + jnp.minimum(count, CAP - 1)
            places = jnp.where(lane == jnp.where(mine, spot, -1), slot, places)
            count = count + mine.astype(jnp.int32)
        return places

    line[...] = lax.fori_loop(0, n, settle_places, jnp.zeros((1, 128), jnp.int32))
    fetch_place = pltpu.make_async_copy(line, place, table_sem.at[3])
    fetch_place.start()

    @pl.when(has_fine)
    def _():
        for k in range(n):
            coarse_arrival(k).wait_recv()
        fetch_fine = pltpu.make_async_copy(fine_tabs, fine_local, table_sem.at[4])
        fetch_fine.start()
        fetch_fine.wait()

    empty = CAP * n

    def settle_octants(source, codes):
        count = jnp.int32(0)
        for b in range(blocks):
            home, spot = split(fine_local[source, 0, b], blocks)
            owner, code = split(fine_local[home, 0, blocks + spot], 8 * blocks)
            mine = owner == me
            hit = jnp.logical_and(mine, fine_local[home, 0, 2 * blocks + spot] == 1)
            slot = CAP * source + jnp.minimum(count, CAP - 1)
            codes = jnp.where(lane == jnp.where(hit, code, -1), slot, codes)
            count = count + mine.astype(jnp.int32)
        return codes

    rounds = jnp.where(has_fine, n, 0)
    line2[...] = lax.fori_loop(0, rounds, settle_octants, jnp.full((1, 128), empty, jnp.int32))
    fetch_octants = pltpu.make_async_copy(line2, octants, table_sem.at[5])
    fetch_octants.start()
    got_ghost[empty] = jnp.zeros(got_ghost.shape[1:], jnp.bfloat16)
    fetch_place.wait()
    fetch_octants.wait()

    wide_lane = lax.broadcasted_iota(jnp.int32, (blocks, 128), 1)
    deep = lax.bitwise_and(wide_lane, 16) != 0
    for corner in range(4):
        mask = jnp.zeros((blocks, 128), jnp.int32)
        for q in range(blocks):
            near_half = (octants[0, q * 8 + corner * 2] < empty).astype(jnp.int32)
            far_half = (octants[0, q * 8 + corner * 2 + 1] < empty).astype(jnp.int32)
            mask = jnp.where(sublane == q, jnp.where(deep, far_half, near_half), mask)
        masks[corner] = mask

    def scatter(part):
        for k in range(1, n):
            block_arrival(part, k).wait_recv()

        def one(q, carry):
            block = gots[part][place[0, q]].astype(jnp.float32)
            for c in range(3):
                at = c * spread + part * piece * blocks + q
                rows[pl.ds(at, piece, stride=blocks), :] = block[c * piece:(c + 1) * piece, :]
            return carry

        lax.fori_loop(0, blocks, one, 0)

    def out_copy(part):
        span = pl.ds(part * SPAN * PLANE, SPAN * PLANE)
        return pltpu.make_async_copy(result.at[:, :, span], out.at[:, :, span], out_sem.at[part])

    def finish(part):
        flagged = [masks[(part * SPAN // 16) * 2 + oy] != 0 for oy in range(2)]

        def one(i, carry):
            x = part * SPAN + i
            for c in range(3):
                for j in range(LANE_TILES):
                    at = c * spread + (x * LANE_TILES + j) * blocks
                    spot = pl.ds(pl.multiple_of(at, blocks), blocks)
                    value = jnp.where(flagged[j // 4], patch[spot, :], rows[spot, :])
                    to = pl.multiple_of(x * PLANE + j * 128, 128)
                    result[c, :, pl.ds(to, 128)] = value.astype(jnp.bfloat16)
            return carry

        lax.fori_loop(0, SPAN, one, 0)
        out_copy(part).start()

    scatter(ORDER[0])
    scatter(ORDER[1])

    @pl.when(has_fine)
    def _():
        for k in range(n):
            ghost_arrival(k).wait_recv()

        def expand(i, carry):
            q, corner = split(i, 4)
            ox, oy = split(corner, 2)
            at = q * 8 + corner * 2
            pair = jnp.concatenate([got_ghost[octants[0, at]], got_ghost[octants[0, at + 1]]], axis=1)
            full = jnp.dot(pair, grow[...], preferred_element_type=jnp.float32)
            for c in range(3):
                for jj in range(4):
                    for half in range(2):
                        x, j = ox * 16 + half * 8, oy * 4 + jj
                        to = c * spread + (x * LANE_TILES + j) * blocks + q
                        patch[pl.ds(to, 8, stride=LANE_TILES * blocks), :] = full[
                            (c * 4 + jj) * 8:(c * 4 + jj + 1) * 8, half * 128:(half + 1) * 128
                        ]
            return carry

        lax.fori_loop(0, 4 * blocks, expand, 0)

    finish(ORDER[0])
    finish(ORDER[1])
    for part in ORDER[2:]:
        scatter(part)
        finish(part)

    @pl.when(not_last)
    def _():
        high(after).wait_send()

    @pl.when(not_first)
    def _():
        low(before).wait_send()

    for k in range(1, n):
        near(k).wait_send()
        for part in ORDER:
            block_copy(part, k).wait_send()

    @pl.when(has_coarse)
    def _():
        for k in range(n):
            coarse(k).wait_send()
            ghost_copy(k).wait_send()

    for part in ORDER:
        out_copy(part).wait()


def selection_tables():
    k = np.arange(1024)
    half, dx, odd, y, z = k // 512, k // 256 % 2, k // 128 % 2, k % 128 // 32, k % 32
    target = half * 64 + (2 * odd + y // 2) * 16 + z // 2
    shrink = np.where(target[:, None] == np.arange(128)[None, :], 0.125, 0.0)
    k = np.arange(256)
    oz, half, y, z = k // 128, k % 128 // 64, k % 64 // 16, k % 16
    target = half * 128 + y * 32 + oz * 16 + z
    grow = np.where(target[:, None] == np.arange(256)[None, :], 1.0, 0.0)
    return shrink, grow


def body(n, levels, vorticity, shift_field, new_index, parent_slot, flags):
    blocks, cells = vorticity.shape[2:]
    vort, shift = vorticity[0], shift_field[0]
    any_space = pl.BlockSpec(memory_space=pl.ANY)
    bf16, f32, i32 = jnp.bfloat16, jnp.float32, jnp.int32
    dma, vm, smem = pltpu.SemaphoreType.DMA, pltpu.VMEM, pltpu.SMEM
    spread = EDGE * LANE_TILES * blocks
    piece = 3 * SPAN * LANE_TILES
    parts = EDGE // SPAN
    shrink, grow = selection_tables()
    out = pl.pallas_call(
        functools.partial(kernel, n, levels),
        out_shape=jax.ShapeDtypeStruct((3, blocks, cells), bf16),
        in_specs=[any_space] * 7,
        out_specs=any_space,
        scratch_shapes=[
            smem((1, blocks), i32), smem((1, blocks), i32), smem((1, blocks), i32),
            vm((4, blocks, cells), bf16), vm(shrink.shape, bf16), vm(grow.shape, bf16),
            vm((3 * spread, 128), f32), vm((3 * spread, 128), f32),
            vm((parts, blocks, piece, 128), bf16), vm((4, blocks, 128), i32), vm((3, blocks, cells), bf16),
            *[vm((n, CAP, piece, 128), bf16)] * parts,
            *[vm((n * CAP, piece, 128), bf16)] * parts,
            vm((blocks, 96, 128), bf16), vm((n, CAP, 96, 128), bf16), vm((n * CAP + 1, 96, 128), bf16),
            vm((128, 128), f32), vm((64, 128), bf16), vm((64, 128), bf16),
            vm((64, 128), bf16), vm((64, 128), bf16), vm((64, 128), f32), vm((64, 128), f32),
            vm((1, 128), i32), vm((n, 1, 128), i32), vm((n, 1, 128), i32),
            smem((n, 1, 128), i32), smem((n, 1, 128), i32),
            vm((1, 128), i32), smem((1, 128), i32), vm((1, 128), i32), smem((1, 128), i32),
            smem((CAP * n,), i32), smem((CAP * n,), i32),
            dma((6,)), dma((3,)), dma((6,)), dma((2,)), dma((2,)), dma((n,)), dma((n,)), dma((n,)), dma((n,)),
            dma((parts, n)), dma((parts, n)), dma((n,)), dma((n,)), dma((parts,)),
            pltpu.SemaphoreType.REGULAR,
        ],
        compiler_params=pltpu.CompilerParams(
            collective_id=0, has_side_effects=True, vmem_limit_bytes=VMEM_LIMIT
        ),
        name="move",
    )(new_index, parent_slot, flags, vort, shift, jnp.asarray(shrink, bf16), jnp.asarray(grow, bf16))
    return out[None]


def solution(mesh):
    placed = (
        P("lvl", None, "blk", None),
        P("lvl", "blk", None),
        P("lvl", "blk"),
        P("lvl", "blk"),
        P("lvl", "blk"),
    )
    step = functools.partial(body, mesh.shape["blk"], mesh.shape["lvl"])
    return jax.shard_map(
        step, mesh=mesh, in_specs=placed, out_specs=P("lvl", None, "blk", None), check_vma=False
    )
```

profile of v0, /device:TPU:9, one launch (start us, length us, event | category | flops | bytes accessed | tf_op | source)
XLA Modules:
  0.0 48.6 jit_solution(17431414437360247751)
XLA Ops:
  0.0 45.9 %move.1 = bf16[3,8,32768]{2,1,0:T(8,128)(2,1)} custom-call(s32[1,8]{1,0:T(1,128)} %spots_in.1, s32[1,8]{1,0:T(1,128)} %parents_in.1, s32[1,8]{1,0:T(1,128)} %flags_in.1, bf16[3,8,32768]{2,1,0:T(8,128)(2,1)} %bitcast.4, bf16[8,32768]{1,0:T(8,128)(2,1)} %bitcast.5, bf16[1024,128]{1,0:T(8,128)(2,1)} %constant.4.clone.shrink_in, ...), custom_call_target="tpu_custom_call" | custom-call | tf_op jit(solution)/shard_map/move/pallas_call | solution.py:526
  45.9 2.7 %copy.9 = bf16[1,3,8,32768]{3,2,1,0:T(8,128)(2,1)} copy(bf16[1,3,8,32768]{3,2,1,0:T(8,128)(2,1)} %bitcast.3) | data formatting | bytes 3145728
where the time goes:
time: 49.5 us; the launch traced here: 48.6 us
  Pallas kernels  45.9 us (93%)
  local copies, waits for them, and re-layouts  2.65 us (5%)
    pallas_call x1, Pallas kernels, body(): pl.pallas_call(functools.partial(kernel, n, levels), out_shape=jax.ShapeD...  45.9 us
    unnamed x1, local copies, waits for them, and re-layouts  2.65 us

commit v1 on v0

--- a/solution.py
+++ b/solution.py
@@ -15,7 +15,7 @@
 CAP = 2
 SPAN = 8
 ORDER = (1, 2, 0, 3)
-VMEM_LIMIT = 60 * 1024 * 1024
+VMEM_LIMIT = 44 * 1024 * 1024
 PIECES = ((4 * PLANE, 20 * PLANE), (20 * PLANE, 32 * PLANE), (0, 4 * PLANE))
 
 
@@ -66,14 +66,14 @@
 
 def kernel(n, levels, spots_in, parents_in, flags_in, vort_in, shift_in, shrink_in, grow_in, out,
            spots, parent_slot, flags, field, shrink, grow,
-           rows, patch, whole, masks, result,
+           rows, patch, whole, masks,
            send0, send1, send2, send3, got0, got1, got2, got3,
-           small, ghost, got_ghost,
+           small, ghost, relay, got_ghost,
            edge, edge_low, edge_high, below, above, halo_low, halo_high,
            tab, near_tabs, fine_tabs, near_local, fine_local, line, place, line2, octants,
            pick, pick_ghost,
-           in_sem, index_sem, table_sem, halo_s, halo_r, near_s, near_r, coarse_s, coarse_r,
-           block_s, block_r, ghost_s, ghost_r, out_sem, ready):
+           in_sem, index_sem, table_sem, halo_s, halo_r, near_s, near_r, down_s, down_r,
+           block_s, block_r, ghost_s, ghost_r, relay_s, relay_r):
     me = lax.axis_index("blk")
     lvl = lax.axis_index("lvl")
     blocks = out.shape[1]
@@ -84,6 +84,7 @@
     sends, gots = (send0, send1, send2, send3), (got0, got1, got2, got3)
     after = device(lax.rem(me + 1, n), lvl)
     before = device(lax.rem(me + n - 1, n), lvl)
+    below_level = device(me, coarse_level)
     has_coarse, has_fine = lvl > 0, lvl < levels - 1
     not_first, not_last = me > 0, me < n - 1
 
@@ -202,21 +203,22 @@
     def near_arrival(k):
         return remote(tab, near_tabs.at[lax.rem(me + n - k, n)], near_s.at[k], near_r.at[k], before)
 
-    def coarse(k):
-        return remote(tab, fine_tabs.at[me], coarse_s.at[k], coarse_r.at[k],
-                      device(lax.rem(me + k, n), coarse_level))
-
-    def coarse_arrival(k):
-        return remote(tab, fine_tabs.at[lax.rem(me + n - k, n)], coarse_s.at[k], coarse_r.at[k], before)
+    def down():
+        return remote(near_tabs, fine_tabs, down_s, down_r, below_level)
 
     def ghost_copy(k):
         to = lax.rem(me + k, n)
-        return remote(ghost.at[to], got_ghost.at[pl.ds(CAP * me, CAP)], ghost_s.at[k], ghost_r.at[k],
-                      device(to, coarse_level))
+        return remote(ghost.at[to], relay.at[pl.ds(CAP * me, CAP)], ghost_s.at[k], ghost_r.at[k], device(to, lvl))
 
     def ghost_arrival(k):
         source = lax.rem(me + n - k, n)
-        return remote(ghost.at[me], got_ghost.at[pl.ds(CAP * source, CAP)], ghost_s.at[k], ghost_r.at[k], before)
+        return remote(ghost.at[me], relay.at[pl.ds(CAP * source, CAP)], ghost_s.at[k], ghost_r.at[k], before)
+
+    def relay_copy(k):
+        source = lax.rem(me + n - k, n)
+        pair = pl.ds(CAP * source, CAP)
+        origin = ghost.at[me] if k == 0 else relay.at[pair]
+        return remote(origin, got_ghost.at[pair], relay_s.at[k], relay_r.at[k], below_level)
 
     def high(target):
         return remote(edge_high, below, halo_s.at[0], halo_r.at[0], target)
@@ -276,10 +278,6 @@
         near(k).start()
     send_blocks(ORDER[0])
 
-    @pl.when(has_fine)
-    def _():
-        pl.semaphore_signal(ready, inc=1, device_id=device(me, fine_level), device_id_type=MESH)
-
     keep(ORDER[0])
     remesh(ORDER[1])
     pack(ORDER[1])
@@ -299,17 +297,15 @@
     for part in ORDER[2:]:
         remesh(part)
         pack(part)
-        send_blocks(part)
         keep(part)
-
-    @pl.when(has_coarse)
-    def _():
-        pl.semaphore_wait(ready, 1)
-        for k in range(n):
-            coarse(k).start()
 
     for k in range(1, n):
         near_arrival(k).wait_recv()
+
+    @pl.when(has_coarse)
+    def _():
+        down().start()
+
     fetch_near = pltpu.make_async_copy(near_tabs, near_local, table_sem.at[2])
     fetch_near.start()
     fetch_near.wait()
@@ -355,8 +351,12 @@
             return carry
 
         lax.fori_loop(0, n, pack_ghost, 0)
-        for k in range(n):
+        for k in range(1, n):
             ghost_copy(k).start()
+        relay_copy(0).start()
+
+    for part in ORDER[2:]:
+        send_blocks(part)
 
     def settle_places(source, places):
         count = jnp.int32(0)
@@ -374,8 +374,7 @@
 
     @pl.when(has_fine)
     def _():
-        for k in range(n):
-            coarse_arrival(k).wait_recv()
+        down().wait_recv()
         fetch_fine = pltpu.make_async_copy(fine_tabs, fine_local, table_sem.at[4])
         fetch_fine.start()
         fetch_fine.wait()
@@ -425,10 +424,6 @@
 
         lax.fori_loop(0, blocks, one, 0)
 
-    def out_copy(part):
-        span = pl.ds(part * SPAN * PLANE, SPAN * PLANE)
-        return pltpu.make_async_copy(result.at[:, :, span], out.at[:, :, span], out_sem.at[part])
-
     def finish(part):
         flagged = [masks[(part * SPAN // 16) * 2 + oy] != 0 for oy in range(2)]
 
@@ -440,19 +435,26 @@
                     spot = pl.ds(pl.multiple_of(at, blocks), blocks)
                     value = jnp.where(flagged[j // 4], patch[spot, :], rows[spot, :])
                     to = pl.multiple_of(x * PLANE + j * 128, 128)
-                    result[c, :, pl.ds(to, 128)] = value.astype(jnp.bfloat16)
+                    out[c, :, pl.ds(to, 128)] = value.astype(jnp.bfloat16)
             return carry
 
         lax.fori_loop(0, SPAN, one, 0)
-        out_copy(part).start()
 
     scatter(ORDER[0])
     scatter(ORDER[1])
 
+    @pl.when(has_coarse)
+    def _():
+        for k in range(1, n):
+            ghost_arrival(k).wait_recv()
+            relay_copy(k).start()
+
+    scatter(ORDER[2])
+
     @pl.when(has_fine)
     def _():
         for k in range(n):
-            ghost_arrival(k).wait_recv()
+            relay_copy(k).wait_recv()
 
         def expand(i, carry):
             q, corner = split(i, 4)
@@ -472,11 +474,10 @@
 
         lax.fori_loop(0, 4 * blocks, expand, 0)
 
-    finish(ORDER[0])
-    finish(ORDER[1])
-    for part in ORDER[2:]:
-        scatter(part)
+    for part in ORDER[:3]:
         finish(part)
+    scatter(ORDER[3])
+    finish(ORDER[3])
 
     @pl.when(not_last)
     def _():
@@ -493,12 +494,11 @@
 
     @pl.when(has_coarse)
     def _():
+        down().wait_send()
+        for k in range(1, n):
+            ghost_copy(k).wait_send()
         for k in range(n):
-            coarse(k).wait_send()
-            ghost_copy(k).wait_send()
-
-    for part in ORDER:
-        out_copy(part).wait()
+            relay_copy(k).wait_send()
 
 
 def selection_tables():
@@ -516,7 +516,8 @@
 def body(n, levels, vorticity, shift_field, new_index, parent_slot, flags):
     blocks, cells = vorticity.shape[2:]
     vort, shift = vorticity[0], shift_field[0]
-    any_space = pl.BlockSpec(memory_space=pl.ANY)
+    hbm = pl.BlockSpec(memory_space=pltpu.HBM)
+    vmem = pl.BlockSpec(memory_space=pltpu.VMEM)
     bf16, f32, i32 = jnp.bfloat16, jnp.float32, jnp.int32
     dma, vm, smem = pltpu.SemaphoreType.DMA, pltpu.VMEM, pltpu.SMEM
     spread = EDGE * LANE_TILES * blocks
@@ -526,31 +527,34 @@
     out = pl.pallas_call(
         functools.partial(kernel, n, levels),
         out_shape=jax.ShapeDtypeStruct((3, blocks, cells), bf16),
-        in_specs=[any_space] * 7,
-        out_specs=any_space,
+        in_specs=[hbm] * 7,
+        out_specs=vmem,
         scratch_shapes=[
             smem((1, blocks), i32), smem((1, blocks), i32), smem((1, blocks), i32),
             vm((4, blocks, cells), bf16), vm(shrink.shape, bf16), vm(grow.shape, bf16),
             vm((3 * spread, 128), f32), vm((3 * spread, 128), f32),
-            vm((parts, blocks, piece, 128), bf16), vm((4, blocks, 128), i32), vm((3, blocks, cells), bf16),
+            vm((parts, blocks, piece, 128), bf16), vm((4, blocks, 128), i32),
             *[vm((n, CAP, piece, 128), bf16)] * parts,
             *[vm((n * CAP, piece, 128), bf16)] * parts,
-            vm((blocks, 96, 128), bf16), vm((n, CAP, 96, 128), bf16), vm((n * CAP + 1, 96, 128), bf16),
+            vm((blocks, 96, 128), bf16), vm((n, CAP, 96, 128), bf16), vm((n * CAP, 96, 128), bf16),
+            vm((n * CAP + 1, 96, 128), bf16),
             vm((128, 128), f32), vm((64, 128), bf16), vm((64, 128), bf16),
             vm((64, 128), bf16), vm((64, 128), bf16), vm((64, 128), f32), vm((64, 128), f32),
             vm((1, 128), i32), vm((n, 1, 128), i32), vm((n, 1, 128), i32),
             smem((n, 1, 128), i32), smem((n, 1, 128), i32),
             vm((1, 128), i32), smem((1, 128), i32), vm((1, 128), i32), smem((1, 128), i32),
             smem((CAP * n,), i32), smem((CAP * n,), i32),
-            dma((6,)), dma((3,)), dma((6,)), dma((2,)), dma((2,)), dma((n,)), dma((n,)), dma((n,)), dma((n,)),
-            dma((parts, n)), dma((parts, n)), dma((n,)), dma((n,)), dma((parts,)),
-            pltpu.SemaphoreType.REGULAR,
+            dma((6,)), dma((3,)), dma((6,)), dma((2,)), dma((2,)), dma((n,)), dma((n,)), dma, dma,
+            dma((parts, n)), dma((parts, n)), dma((n,)), dma((n,)), dma((n,)), dma((n,)),
         ],
         compiler_params=pltpu.CompilerParams(
             collective_id=0, has_side_effects=True, vmem_limit_bytes=VMEM_LIMIT
         ),
         name="move",
-    )(new_index, parent_slot, flags, vort, shift, jnp.asarray(shrink, bf16), jnp.asarray(grow, bf16))
+    )(*[
+        pltpu.with_memory_space_constraint(x, pltpu.HBM)
+        for x in (new_index, parent_slot, flags, vort, shift, jnp.asarray(shrink, bf16), jnp.asarray(grow, bf16))
+    ])
     return out[None]
 
 

time: 49.5 us -> 46.2 us (0.933); the launches traced: 48.6 us -> 46.1 us
  local copies, waits for them, and re-layouts: 2.65 us -> 1.15 us
  Pallas kernels: 45.9 us -> 44.9 us
    unnamed x1, local copies, waits for them, and re-layouts: 2.65 us -> 1.15 us
    pallas_call x1, Pallas kernels: 45.9 us -> 44.9 us  [body(): pl.pallas_call(functools.partial(kernel, n, levels), out_shape=jax.ShapeD...]
where the time goes in v1:
time: 46.2 us; the launch traced here: 46.1 us
  Pallas kernels  44.9 us (97%)
  local copies, waits for them, and re-layouts  1.15 us (2%)
    pallas_call x1, Pallas kernels, body(): pl.pallas_call(functools.partial(kernel, n, levels), out_shape=jax.ShapeD...  44.9 us
    unnamed x1, local copies, waits for them, and re-layouts  1.15 us

profile of v1, /device:TPU:9, one launch (start us, length us, event | category | flops | bytes accessed | tf_op | source)
XLA Modules:
  0.0 46.1 jit_solution(12012086374938269855)
XLA Ops:
  0.0 44.9 %move.1 = bf16[3,8,32768]{2,1,0:T(8,128)(2,1)S(1)} custom-call(s32[1,8]{1,0:T(1,128)} %spots_in.1, s32[1,8]{1,0:T(1,128)} %parents_in.1, s32[1,8]{1,0:T(1,128)} %flags_in.1, bf16[3,8,32768]{2,1,0:T(8,128)(2,1)} %bitcast.4, bf16[8,32768]{1,0:T(8,128)(2,1)} %bitcast.5, bf16[1024,128]{1,0:T(8,128)(2,1)} %constant.4.clone.shrink_in, ...), custom_call_target="tpu_custom_call" | custom-call | tf_op jit(solution)/shard_map/move/pallas_call | solution.py:527
  44.9 1.1 %copy.9 = bf16[1,3,8,32768]{3,2,1,0:T(8,128)(2,1)} copy(bf16[1,3,8,32768]{3,2,1,0:T(8,128)(2,1)S(1)} %bitcast.3) | data formatting | bytes 3145728

commit v2 on v1

--- a/solution.py
+++ b/solution.py
@@ -64,6 +64,29 @@
     return first, second
 
 
+def flip(value, mask):
+    for bit in range(mask.bit_length()):
+        if mask >> bit & 1:
+            value = value + (1 << bit) * (1 - 2 * lax.rem(lax.div(value, 1 << bit), 2))
+    return value
+
+
+def groups(n):
+    others = range(1, n)
+    if n < 8 or n & (n - 1):
+        return list(others), [], []
+    bits = n.bit_length() - 1
+    across = ((1 << (bits - 1) // 2) - 1) << 1
+    along = (n - 1) & ~across & ~1
+    far = [k for k in others if k & across and k & along]
+    close = sorted((k for k in others if k not in far), key=lambda k: (k == 1, k & 1, k))
+    return close, far, [k for k in others if k & ~across == 0]
+
+
+def shared_rows(lvl, levels):
+    return 16 * min(max(round(6 * lvl / levels), 1), 5)
+
+
 def kernel(n, levels, spots_in, parents_in, flags_in, vort_in, shift_in, shrink_in, grow_in, out,
            spots, parent_slot, flags, field, shrink, grow,
            rows, patch, whole, masks,
@@ -73,12 +96,14 @@
            tab, near_tabs, fine_tabs, near_local, fine_local, line, place, line2, octants,
            pick, pick_ghost,
            in_sem, index_sem, table_sem, halo_s, halo_r, near_s, near_r, down_s, down_r,
-           block_s, block_r, ghost_s, ghost_r, relay_s, relay_r):
+           block_s, block_r, ghost_s, ghost_r, relay_s, relay_r, direct_s, direct_r,
+           cross_ready, plane_ready):
     me = lax.axis_index("blk")
     lvl = lax.axis_index("lvl")
     blocks = out.shape[1]
     spread = EDGE * LANE_TILES * blocks
     piece = SPAN * LANE_TILES
+    pitch = (LANE_TILES + 1) * blocks
     coarse_level = jnp.maximum(lvl - 1, 0)
     fine_level = jnp.minimum(lvl + 1, levels - 1)
     sends, gots = (send0, send1, send2, send3), (got0, got1, got2, got3)
@@ -88,17 +113,21 @@
     has_coarse, has_fine = lvl > 0, lvl < levels - 1
     not_first, not_last = me > 0, me < n - 1
 
+    close, far, cross = groups(n)
+    everyone = close + far
+    if n & (n - 1):
+        partners = [lax.rem(me + k, n) for k in range(n)]
+        sources = [lax.rem(me + n - k, n) for k in range(n)]
+    else:
+        partners = sources = [flip(me, k) for k in range(n)]
+
     barrier = pltpu.get_barrier_semaphore()
 
     def greet(blk, level):
         pl.semaphore_signal(barrier, inc=1, device_id=device(blk, level), device_id_type=MESH)
 
-    for k in range(1, n):
-        greet(lax.rem(me + k, n), lvl)
-
-    @pl.when(has_coarse)
-    def _():
-        greet(me, coarse_level)
+    for k in close:
+        greet(partners[k], lvl)
 
     @pl.when(has_fine)
     def _():
@@ -171,54 +200,68 @@
                 ].astype(jnp.bfloat16)
 
     def pack(part):
-        def one(k, carry):
-            to = lax.rem(me + k, n)
+        def one(to, carry):
             for s in range(CAP):
                 sends[part][to, s] = whole[part, pick[CAP * to + s]]
             return carry
 
-        lax.fori_loop(1, n, one, 0)
+        lax.fori_loop(0, n, one, 0)
 
     def keep(part):
         for s in range(CAP):
             gots[part][CAP * me + s] = whole[part, pick[CAP * me + s]]
 
     def block_copy(part, k):
-        to = lax.rem(me + k, n)
+        to = partners[k]
         return remote(sends[part].at[to], gots[part].at[pl.ds(CAP * me, CAP)],
                       block_s.at[part, k], block_r.at[part, k], device(to, lvl))
 
     def block_arrival(part, k):
-        source = lax.rem(me + n - k, n)
+        source = sources[k]
         return remote(sends[part].at[me], gots[part].at[pl.ds(CAP * source, CAP)],
                       block_s.at[part, k], block_r.at[part, k], before)
 
-    def send_blocks(part):
-        for k in range(1, n):
+    def send_blocks(part, group):
+        for k in group:
             block_copy(part, k).start()
 
     def near(k):
-        return remote(tab, near_tabs.at[me], near_s.at[k], near_r.at[k], device(lax.rem(me + k, n), lvl))
+        return remote(tab, near_tabs.at[me], near_s.at[k], near_r.at[k], device(partners[k], lvl))
 
     def near_arrival(k):
-        return remote(tab, near_tabs.at[lax.rem(me + n - k, n)], near_s.at[k], near_r.at[k], before)
+        return remote(tab, near_tabs.at[sources[k]], near_s.at[k], near_r.at[k], before)
 
     def down():
         return remote(near_tabs, fine_tabs, down_s, down_r, below_level)
 
-    def ghost_copy(k):
-        to = lax.rem(me + k, n)
-        return remote(ghost.at[to], relay.at[pl.ds(CAP * me, CAP)], ghost_s.at[k], ghost_r.at[k], device(to, lvl))
-
-    def ghost_arrival(k):
-        source = lax.rem(me + n - k, n)
-        return remote(ghost.at[me], relay.at[pl.ds(CAP * source, CAP)], ghost_s.at[k], ghost_r.at[k], before)
-
-    def relay_copy(k):
-        source = lax.rem(me + n - k, n)
-        pair = pl.ds(CAP * source, CAP)
-        origin = ghost.at[me] if k == 0 else relay.at[pair]
-        return remote(origin, got_ghost.at[pair], relay_s.at[k], relay_r.at[k], below_level)
+    def ghost_copy(k, size):
+        part = pl.ds(0, size)
+        return remote(ghost.at[partners[k], :, part], relay.at[pl.ds(CAP * me, CAP), part],
+                      ghost_s.at[k], ghost_r.at[k], device(partners[k], lvl))
+
+    def ghost_arrival(k, size):
+        part = pl.ds(0, size)
+        return remote(ghost.at[me, :, part], relay.at[pl.ds(CAP * sources[k], CAP), part],
+                      ghost_s.at[k], ghost_r.at[k], before)
+
+    def relay_copy(k, size):
+        pair, part = pl.ds(CAP * sources[k], CAP), pl.ds(0, size)
+        origin = ghost.at[me, :, part] if k == 0 else relay.at[pair, part]
+        return remote(origin, got_ghost.at[pair, part], relay_s.at[k], relay_r.at[k], below_level)
+
+    def direct_copy(k, size):
+        part = pl.ds(size, 96 - size)
+        return remote(ghost.at[partners[k], :, part], got_ghost.at[pl.ds(CAP * me, CAP), part],
+                      direct_s.at[k], direct_r.at[k], device(partners[k], coarse_level))
+
+    def direct_arrival(k, size):
+        part = pl.ds(size, 96 - size)
+        return remote(ghost.at[me, :, part], got_ghost.at[pl.ds(CAP * sources[k], CAP), part],
+                      direct_s.at[k], direct_r.at[k], before)
+
+    def on_level(shift, action):
+        for level in range(1, levels):
+            pl.when(lvl == level - shift)(functools.partial(action, shared_rows(level, levels)))
 
     def high(target):
         return remote(edge_high, below, halo_s.at[0], halo_r.at[0], target)
@@ -263,8 +306,14 @@
     edge_low[...] = edge[0:64, :].astype(jnp.bfloat16)
     edge_high[...] = edge[64:128, :].astype(jnp.bfloat16)
 
-    nearby = n - 1 + has_coarse.astype(jnp.int32) + has_fine.astype(jnp.int32)
-    pl.semaphore_wait(barrier, nearby)
+    pl.semaphore_wait(barrier, len(close) + has_coarse.astype(jnp.int32))
+    for k in cross:
+        pl.semaphore_signal(cross_ready, inc=1, device_id=device(partners[k], lvl), device_id_type=MESH)
+    for k in close:
+        near(k).start()
+    send_blocks(ORDER[0], close)
+    if cross:
+        pl.semaphore_wait(cross_ready, len(cross))
 
     @pl.when(not_last)
     def _():
@@ -274,14 +323,13 @@
     def _():
         low(before).start()
 
-    for k in range(1, n):
+    for k in far:
         near(k).start()
-    send_blocks(ORDER[0])
-
+    send_blocks(ORDER[0], far)
     keep(ORDER[0])
     remesh(ORDER[1])
     pack(ORDER[1])
-    send_blocks(ORDER[1])
+    send_blocks(ORDER[1], everyone)
     keep(ORDER[1])
 
     @pl.when(not_last)
@@ -351,12 +399,15 @@
             return carry
 
         lax.fori_loop(0, n, pack_ghost, 0)
-        for k in range(1, n):
-            ghost_copy(k).start()
-        relay_copy(0).start()
-
+
+    def share(size):
+        for k in everyone:
+            ghost_copy(k, size).start()
+        relay_copy(0, size).start()
+
+    on_level(0, share)
     for part in ORDER[2:]:
-        send_blocks(part)
+        send_blocks(part, everyone)
 
     def settle_places(source, places):
         count = jnp.int32(0)
@@ -375,10 +426,20 @@
     @pl.when(has_fine)
     def _():
         down().wait_recv()
+        pl.semaphore_signal(plane_ready, inc=1, device_id=device(me, fine_level), device_id_type=MESH)
         fetch_fine = pltpu.make_async_copy(fine_tabs, fine_local, table_sem.at[4])
         fetch_fine.start()
         fetch_fine.wait()
 
+    @pl.when(has_coarse)
+    def _():
+        pl.semaphore_wait(plane_ready, 1)
+
+    def rest(size):
+        for k in [0] + everyone:
+            direct_copy(k, size).start()
+
+    on_level(0, rest)
     empty = CAP * n
 
     def settle_octants(source, codes):
@@ -431,9 +492,9 @@
             x = part * SPAN + i
             for c in range(3):
                 for j in range(LANE_TILES):
-                    at = c * spread + (x * LANE_TILES + j) * blocks
-                    spot = pl.ds(pl.multiple_of(at, blocks), blocks)
-                    value = jnp.where(flagged[j // 4], patch[spot, :], rows[spot, :])
+                    at = pl.multiple_of(c * spread + (x * LANE_TILES + j) * blocks, blocks)
+                    over = pl.multiple_of((c * EDGE + x) * pitch + j * blocks, blocks)
+                    value = jnp.where(flagged[j // 4], patch[pl.ds(over, blocks), :], rows[pl.ds(at, blocks), :])
                     to = pl.multiple_of(x * PLANE + j * 128, 128)
                     out[c, :, pl.ds(to, 128)] = value.astype(jnp.bfloat16)
             return carry
@@ -443,36 +504,39 @@
     scatter(ORDER[0])
     scatter(ORDER[1])
 
-    @pl.when(has_coarse)
-    def _():
-        for k in range(1, n):
-            ghost_arrival(k).wait_recv()
-            relay_copy(k).start()
-
+    def forward(size):
+        for k in everyone:
+            ghost_arrival(k, size).wait_recv()
+            relay_copy(k, size).start()
+
+    def gather(size):
+        for k in [0] + everyone:
+            relay_copy(k, size).wait_recv()
+            direct_arrival(k, size).wait_recv()
+
+    on_level(0, forward)
     scatter(ORDER[2])
+    on_level(1, gather)
 
     @pl.when(has_fine)
     def _():
-        for k in range(n):
-            relay_copy(k).wait_recv()
-
-        def expand(i, carry):
-            q, corner = split(i, 4)
-            ox, oy = split(corner, 2)
-            at = q * 8 + corner * 2
-            pair = jnp.concatenate([got_ghost[octants[0, at]], got_ghost[octants[0, at + 1]]], axis=1)
-            full = jnp.dot(pair, grow[...], preferred_element_type=jnp.float32)
-            for c in range(3):
-                for jj in range(4):
-                    for half in range(2):
-                        x, j = ox * 16 + half * 8, oy * 4 + jj
-                        to = c * spread + (x * LANE_TILES + j) * blocks + q
-                        patch[pl.ds(to, 8, stride=LANE_TILES * blocks), :] = full[
-                            (c * 4 + jj) * 8:(c * 4 + jj + 1) * 8, half * 128:(half + 1) * 128
-                        ]
-            return carry
-
-        lax.fori_loop(0, 4 * blocks, expand, 0)
+        def expand(q, carry):
+            pairs = []
+            for corner in range(4):
+                at = q * 8 + corner * 2
+                pairs.append(jnp.concatenate([got_ghost[octants[0, at]], got_ghost[octants[0, at + 1]]], axis=1))
+            full = jnp.dot(jnp.concatenate(pairs, axis=0), grow[...], preferred_element_type=jnp.float32)
+            for corner in range(4):
+                for c in range(3):
+                    for jj in range(4):
+                        for half in range(2):
+                            x, j = corner // 2 * 16 + half * 8, corner % 2 * 4 + jj
+                            to = (c * EDGE + x) * pitch + j * blocks + q
+                            at = (corner * 12 + c * 4 + jj) * 8
+                            patch[pl.ds(to, 8, stride=pitch), :] = full[at:at + 8, half * 128:(half + 1) * 128]
+            return carry
+
+        lax.fori_loop(0, blocks, expand, 0)
 
     for part in ORDER[:3]:
         finish(part)
@@ -495,10 +559,15 @@
     @pl.when(has_coarse)
     def _():
         down().wait_send()
-        for k in range(1, n):
-            ghost_copy(k).wait_send()
-        for k in range(n):
-            relay_copy(k).wait_send()
+
+    def drain(size):
+        for k in everyone:
+            ghost_copy(k, size).wait_send()
+        for k in [0] + everyone:
+            relay_copy(k, size).wait_send()
+            direct_copy(k, size).wait_send()
+
+    on_level(0, drain)
 
 
 def selection_tables():
@@ -532,7 +601,7 @@
         scratch_shapes=[
             smem((1, blocks), i32), smem((1, blocks), i32), smem((1, blocks), i32),
             vm((4, blocks, cells), bf16), vm(shrink.shape, bf16), vm(grow.shape, bf16),
-            vm((3 * spread, 128), f32), vm((3 * spread, 128), f32),
+            vm((3 * spread, 128), f32), vm((3 * EDGE * (LANE_TILES + 1) * blocks, 128), f32),
             vm((parts, blocks, piece, 128), bf16), vm((4, blocks, 128), i32),
             *[vm((n, CAP, piece, 128), bf16)] * parts,
             *[vm((n * CAP, piece, 128), bf16)] * parts,
@@ -545,7 +614,8 @@
             vm((1, 128), i32), smem((1, 128), i32), vm((1, 128), i32), smem((1, 128), i32),
             smem((CAP * n,), i32), smem((CAP * n,), i32),
             dma((6,)), dma((3,)), dma((6,)), dma((2,)), dma((2,)), dma((n,)), dma((n,)), dma, dma,
-            dma((parts, n)), dma((parts, n)), dma((n,)), dma((n,)), dma((n,)), dma((n,)),
+            dma((parts, n)), dma((parts, n)), dma((n,)), dma((n,)), dma((n,)), dma((n,)), dma((n,)), dma((n,)),
+            pltpu.SemaphoreType.REGULAR, pltpu.SemaphoreType.REGULAR,
         ],
         compiler_params=pltpu.CompilerParams(
             collective_id=0, has_side_effects=True, vmem_limit_bytes=VMEM_LIMIT

time: 46.2 us -> 46.7 us (1.011)
  no operation moved by 1% of the time
where the time goes in v2:
time: 46.7 us; the launch traced here: 46.2 us
  Pallas kernels  45.1 us (97%)
  local copies, waits for them, and re-layouts  1.15 us (2%)
    pallas_call x1, Pallas kernels, body(): pl.pallas_call(functools.partial(kernel, n, levels), out_shape=jax.ShapeD...  45.1 us
    unnamed x1, local copies, waits for them, and re-layouts  1.15 us

profile of v2, /device:TPU:9, one launch (start us, length us, event | category | flops | bytes accessed | tf_op | source)
XLA Modules:
  0.0 46.2 jit_solution(3539159148966790558)
XLA Ops:
  0.0 45.1 %move.1 = bf16[3,8,32768]{2,1,0:T(8,128)(2,1)S(1)} custom-call(s32[1,8]{1,0:T(1,128)} %spots_in.1, s32[1,8]{1,0:T(1,128)} %parents_in.1, s32[1,8]{1,0:T(1,128)} %flags_in.1, bf16[3,8,32768]{2,1,0:T(8,128)(2,1)} %bitcast.4, bf16[8,32768]{1,0:T(8,128)(2,1)} %bitcast.5, bf16[1024,128]{1,0:T(8,128)(2,1)} %constant.4.clone.shrink_in, ...), custom_call_target="tpu_custom_call" | custom-call | tf_op jit(solution)/shard_map/move/pallas_call | solution.py:596
  45.1 1.1 %copy.9 = bf16[1,3,8,32768]{3,2,1,0:T(8,128)(2,1)} copy(bf16[1,3,8,32768]{3,2,1,0:T(8,128)(2,1)S(1)} %bitcast.3) | data formatting | bytes 3145728

commit v3 on v2

--- a/solution.py
+++ b/solution.py
@@ -64,27 +64,8 @@
     return first, second
 
 
-def flip(value, mask):
-    for bit in range(mask.bit_length()):
-        if mask >> bit & 1:
-            value = value + (1 << bit) * (1 - 2 * lax.rem(lax.div(value, 1 << bit), 2))
-    return value
-
-
-def groups(n):
-    others = range(1, n)
-    if n < 8 or n & (n - 1):
-        return list(others), [], []
-    bits = n.bit_length() - 1
-    across = ((1 << (bits - 1) // 2) - 1) << 1
-    along = (n - 1) & ~across & ~1
-    far = [k for k in others if k & across and k & along]
-    close = sorted((k for k in others if k not in far), key=lambda k: (k == 1, k & 1, k))
-    return close, far, [k for k in others if k & ~across == 0]
-
-
 def shared_rows(lvl, levels):
-    return 16 * min(max(round(6 * lvl / levels), 1), 5)
+    return 16 * min(max(round(6 * (lvl + 2) / (levels + 2)), 1), 5)
 
 
 def kernel(n, levels, spots_in, parents_in, flags_in, vort_in, shift_in, shrink_in, grow_in, out,
@@ -96,8 +77,7 @@
            tab, near_tabs, fine_tabs, near_local, fine_local, line, place, line2, octants,
            pick, pick_ghost,
            in_sem, index_sem, table_sem, halo_s, halo_r, near_s, near_r, down_s, down_r,
-           block_s, block_r, ghost_s, ghost_r, relay_s, relay_r, direct_s, direct_r,
-           cross_ready, plane_ready):
+           block_s, block_r, ghost_s, ghost_r, relay_s, relay_r, direct_s, direct_r, plane_ready):
     me = lax.axis_index("blk")
     lvl = lax.axis_index("lvl")
     blocks = out.shape[1]
@@ -113,20 +93,16 @@
     has_coarse, has_fine = lvl > 0, lvl < levels - 1
     not_first, not_last = me > 0, me < n - 1
 
-    close, far, cross = groups(n)
-    everyone = close + far
-    if n & (n - 1):
-        partners = [lax.rem(me + k, n) for k in range(n)]
-        sources = [lax.rem(me + n - k, n) for k in range(n)]
-    else:
-        partners = sources = [flip(me, k) for k in range(n)]
+    others = range(1, n)
+    partners = [lax.rem(me + k, n) for k in range(n)]
+    sources = [lax.rem(me + n - k, n) for k in range(n)]
 
     barrier = pltpu.get_barrier_semaphore()
 
     def greet(blk, level):
         pl.semaphore_signal(barrier, inc=1, device_id=device(blk, level), device_id_type=MESH)
 
-    for k in close:
+    for k in others:
         greet(partners[k], lvl)
 
     @pl.when(has_fine)
@@ -211,19 +187,17 @@
         for s in range(CAP):
             gots[part][CAP * me + s] = whole[part, pick[CAP * me + s]]
 
-    def block_copy(part, k):
-        to = partners[k]
+    def block_copy(part, to):
         return remote(sends[part].at[to], gots[part].at[pl.ds(CAP * me, CAP)],
-                      block_s.at[part, k], block_r.at[part, k], device(to, lvl))
-
-    def block_arrival(part, k):
-        source = sources[k]
+                      block_s.at[part, to], block_r.at[part, me], device(to, lvl))
+
+    def block_arrival(part, source):
         return remote(sends[part].at[me], gots[part].at[pl.ds(CAP * source, CAP)],
-                      block_s.at[part, k], block_r.at[part, k], before)
-
-    def send_blocks(part, group):
-        for k in group:
-            block_copy(part, k).start()
+                      block_s.at[part, source], block_r.at[part, source], before)
+
+    def send_blocks(part):
+        for k in others:
+            block_copy(part, partners[k]).start()
 
     def near(k):
         return remote(tab, near_tabs.at[me], near_s.at[k], near_r.at[k], device(partners[k], lvl))
@@ -306,30 +280,23 @@
     edge_low[...] = edge[0:64, :].astype(jnp.bfloat16)
     edge_high[...] = edge[64:128, :].astype(jnp.bfloat16)
 
-    pl.semaphore_wait(barrier, len(close) + has_coarse.astype(jnp.int32))
-    for k in cross:
-        pl.semaphore_signal(cross_ready, inc=1, device_id=device(partners[k], lvl), device_id_type=MESH)
-    for k in close:
+    pl.semaphore_wait(barrier, n - 1 + has_coarse.astype(jnp.int32))
+
+    @pl.when(not_last)
+    def _():
+        high(after).start()
+
+    @pl.when(not_first)
+    def _():
+        low(before).start()
+
+    for k in others:
         near(k).start()
-    send_blocks(ORDER[0], close)
-    if cross:
-        pl.semaphore_wait(cross_ready, len(cross))
-
-    @pl.when(not_last)
-    def _():
-        high(after).start()
-
-    @pl.when(not_first)
-    def _():
-        low(before).start()
-
-    for k in far:
-        near(k).start()
-    send_blocks(ORDER[0], far)
+    send_blocks(ORDER[0])
     keep(ORDER[0])
     remesh(ORDER[1])
     pack(ORDER[1])
-    send_blocks(ORDER[1], everyone)
+    send_blocks(ORDER[1])
     keep(ORDER[1])
 
     @pl.when(not_last)
@@ -347,7 +314,7 @@
         pack(part)
         keep(part)
 
-    for k in range(1, n):
+    for k in others:
         near_arrival(k).wait_recv()
 
     @pl.when(has_coarse)
@@ -401,13 +368,13 @@
         lax.fori_loop(0, n, pack_ghost, 0)
 
     def share(size):
-        for k in everyone:
+        for k in others:
             ghost_copy(k, size).start()
         relay_copy(0, size).start()
 
     on_level(0, share)
     for part in ORDER[2:]:
-        send_blocks(part, everyone)
+        send_blocks(part)
 
     def settle_places(source, places):
         count = jnp.int32(0)
@@ -436,7 +403,7 @@
         pl.semaphore_wait(plane_ready, 1)
 
     def rest(size):
-        for k in [0] + everyone:
+        for k in range(n):
             direct_copy(k, size).start()
 
     on_level(0, rest)
@@ -473,8 +440,8 @@
         masks[corner] = mask
 
     def scatter(part):
-        for k in range(1, n):
-            block_arrival(part, k).wait_recv()
+        for k in others:
+            block_arrival(part, sources[k]).wait_recv()
 
         def one(q, carry):
             block = gots[part][place[0, q]].astype(jnp.float32)
@@ -505,12 +472,12 @@
     scatter(ORDER[1])
 
     def forward(size):
-        for k in everyone:
+        for k in others:
             ghost_arrival(k, size).wait_recv()
             relay_copy(k, size).start()
 
     def gather(size):
-        for k in [0] + everyone:
+        for k in range(n):
             relay_copy(k, size).wait_recv()
             direct_arrival(k, size).wait_recv()
 
@@ -551,19 +518,19 @@
     def _():
         low(before).wait_send()
 
-    for k in range(1, n):
+    for k in others:
         near(k).wait_send()
         for part in ORDER:
-            block_copy(part, k).wait_send()
+            block_copy(part, partners[k]).wait_send()
 
     @pl.when(has_coarse)
     def _():
         down().wait_send()
 
     def drain(size):
-        for k in everyone:
+        for k in others:
             ghost_copy(k, size).wait_send()
-        for k in [0] + everyone:
+        for k in range(n):
             relay_copy(k, size).wait_send()
             direct_copy(k, size).wait_send()
 
@@ -615,7 +582,7 @@
             smem((CAP * n,), i32), smem((CAP * n,), i32),
             dma((6,)), dma((3,)), dma((6,)), dma((2,)), dma((2,)), dma((n,)), dma((n,)), dma, dma,
             dma((parts, n)), dma((parts, n)), dma((n,)), dma((n,)), dma((n,)), dma((n,)), dma((n,)), dma((n,)),
-            pltpu.SemaphoreType.REGULAR, pltpu.SemaphoreType.REGULAR,
+            pltpu.SemaphoreType.REGULAR,
         ],
         compiler_params=pltpu.CompilerParams(
             collective_id=0, has_side_effects=True, vmem_limit_bytes=VMEM_LIMIT

time: 46.7 us -> 45.2 us (0.968)
  Pallas kernels: 45.1 us -> 43.8 us
    pallas_call x1, Pallas kernels: 45.1 us -> 43.8 us  [body(): pl.pallas_call(functools.partial(kernel, n, levels), out_shape=jax.ShapeD...]
where the time goes in v3:
time: 45.2 us; the launch traced here: 45 us
  Pallas kernels  43.8 us (97%)
  local copies, waits for them, and re-layouts  1.15 us (3%)
    pallas_call x1, Pallas kernels, body(): pl.pallas_call(functools.partial(kernel, n, levels), out_shape=jax.ShapeD...  43.8 us
    unnamed x1, local copies, waits for them, and re-layouts  1.15 us

profile of v3, /device:TPU:9, one launch (start us, length us, event | category | flops | bytes accessed | tf_op | source)
XLA Modules:
  0.0 45.0 jit_solution(9342636218589923948)
XLA Ops:
  0.0 43.8 %move.1 = bf16[3,8,32768]{2,1,0:T(8,128)(2,1)S(1)} custom-call(s32[1,8]{1,0:T(1,128)} %spots_in.1, s32[1,8]{1,0:T(1,128)} %parents_in.1, s32[1,8]{1,0:T(1,128)} %flags_in.1, bf16[3,8,32768]{2,1,0:T(8,128)(2,1)} %bitcast.4, bf16[8,32768]{1,0:T(8,128)(2,1)} %bitcast.5, bf16[1024,128]{1,0:T(8,128)(2,1)} %constant.4.clone.shrink_in, ...), custom_call_target="tpu_custom_call" | custom-call | tf_op jit(solution)/shard_map/move/pallas_call | solution.py:563
  43.8 1.1 %copy.9 = bf16[1,3,8,32768]{3,2,1,0:T(8,128)(2,1)} copy(bf16[1,3,8,32768]{3,2,1,0:T(8,128)(2,1)S(1)} %bitcast.3) | data formatting | bytes 3145728

commit v4 on v3

--- a/solution.py
+++ b/solution.py
@@ -13,10 +13,9 @@
 PLANE = EDGE * EDGE
 LANE_TILES = PLANE // 128
 CAP = 2
-SPAN = 8
-ORDER = (1, 2, 0, 3)
+PARTS = ((8, 12), (12, 28), (0, 8), (28, 32))
 VMEM_LIMIT = 44 * 1024 * 1024
-PIECES = ((4 * PLANE, 20 * PLANE), (20 * PLANE, 32 * PLANE), (0, 4 * PLANE))
+PIECES = ((6 * PLANE, 14 * PLANE), (14 * PLANE, 32 * PLANE), (0, 6 * PLANE))
 
 
 def device(blk, lvl):
@@ -70,7 +69,7 @@
 
 def kernel(n, levels, spots_in, parents_in, flags_in, vort_in, shift_in, shrink_in, grow_in, out,
            spots, parent_slot, flags, field, shrink, grow,
-           rows, patch, whole, masks,
+           rows, patch, whole0, whole1, whole2, whole3, masks,
            send0, send1, send2, send3, got0, got1, got2, got3,
            small, ghost, relay, got_ghost,
            edge, edge_low, edge_high, below, above, halo_low, halo_high,
@@ -82,10 +81,11 @@
     lvl = lax.axis_index("lvl")
     blocks = out.shape[1]
     spread = EDGE * LANE_TILES * blocks
-    piece = SPAN * LANE_TILES
     pitch = (LANE_TILES + 1) * blocks
     coarse_level = jnp.maximum(lvl - 1, 0)
     fine_level = jnp.minimum(lvl + 1, levels - 1)
+    pieces = [(x1 - x0) * LANE_TILES for x0, x1 in PARTS]
+    wholes = (whole0, whole1, whole2, whole3)
     sends, gots = (send0, send1, send2, send3), (got0, got1, got2, got3)
     after = device(lax.rem(me + 1, n), lvl)
     before = device(lax.rem(me + n - 1, n), lvl)
@@ -124,11 +124,12 @@
         pltpu.make_async_copy(shrink_in, shrink, table_sem.at[0]),
         pltpu.make_async_copy(grow_in, grow, table_sem.at[1]),
     )
+    for copy in loads[0]:
+        copy.start()
     for copy in index_loads:
         copy.start()
-    for pair in loads:
-        for copy in pair:
-            copy.start()
+    for copy in loads[1] + loads[2]:
+        copy.start()
     for copy in constants:
         copy.start()
 
@@ -149,7 +150,7 @@
         return tile(f, x, j)
 
     def remesh(part):
-        x0, x1 = part * SPAN, (part + 1) * SPAN
+        (x0, x1), piece = PARTS[part], pieces[part]
 
         def chunk(j, carry):
             sums = [{}, {}, {}]
@@ -171,21 +172,21 @@
         for b in range(blocks):
             for c in range(3):
                 at = c * spread + x0 * LANE_TILES * blocks + b
-                whole[part, b, c * piece:(c + 1) * piece, :] = rows[
+                wholes[part][b, c * piece:(c + 1) * piece, :] = rows[
                     pl.ds(at, piece, stride=blocks), :
                 ].astype(jnp.bfloat16)
 
     def pack(part):
         def one(to, carry):
             for s in range(CAP):
-                sends[part][to, s] = whole[part, pick[CAP * to + s]]
+                sends[part][to, s] = wholes[part][pick[CAP * to + s]]
             return carry
 
         lax.fori_loop(0, n, one, 0)
 
     def keep(part):
         for s in range(CAP):
-            gots[part][CAP * me + s] = whole[part, pick[CAP * me + s]]
+            gots[part][CAP * me + s] = wholes[part][pick[CAP * me + s]]
 
     def block_copy(part, to):
         return remote(sends[part].at[to], gots[part].at[pl.ds(CAP * me, CAP)],
@@ -263,8 +264,8 @@
 
     for copy in loads[0]:
         copy.wait()
-    remesh(ORDER[0])
-    pack(ORDER[0])
+    remesh(0)
+    pack(0)
     for copy in loads[1] + loads[2]:
         copy.wait()
 
@@ -282,6 +283,8 @@
 
     pl.semaphore_wait(barrier, n - 1 + has_coarse.astype(jnp.int32))
 
+    send_blocks(0)
+
     @pl.when(not_last)
     def _():
         high(after).start()
@@ -292,12 +295,11 @@
 
     for k in others:
         near(k).start()
-    send_blocks(ORDER[0])
-    keep(ORDER[0])
-    remesh(ORDER[1])
-    pack(ORDER[1])
-    send_blocks(ORDER[1])
-    keep(ORDER[1])
+    keep(0)
+    remesh(1)
+    pack(1)
+    send_blocks(1)
+    keep(1)
 
     @pl.when(not_last)
     def _():
@@ -309,7 +311,7 @@
 
     halo_low[...] = jnp.where(not_first, below[...].astype(jnp.float32), 0.0)
     halo_high[...] = jnp.where(not_last, above[...].astype(jnp.float32), 0.0)
-    for part in ORDER[2:]:
+    for part in (2, 3):
         remesh(part)
         pack(part)
         keep(part)
@@ -373,7 +375,7 @@
         relay_copy(0, size).start()
 
     on_level(0, share)
-    for part in ORDER[2:]:
+    for part in (2, 3):
         send_blocks(part)
 
     def settle_places(source, places):
@@ -443,20 +445,20 @@
         for k in others:
             block_arrival(part, sources[k]).wait_recv()
 
+        piece = pieces[part]
+
         def one(q, carry):
             block = gots[part][place[0, q]].astype(jnp.float32)
             for c in range(3):
-                at = c * spread + part * piece * blocks + q
+                at = c * spread + PARTS[part][0] * LANE_TILES * blocks + q
                 rows[pl.ds(at, piece, stride=blocks), :] = block[c * piece:(c + 1) * piece, :]
             return carry
 
         lax.fori_loop(0, blocks, one, 0)
 
     def finish(part):
-        flagged = [masks[(part * SPAN // 16) * 2 + oy] != 0 for oy in range(2)]
-
-        def one(i, carry):
-            x = part * SPAN + i
+        def one(x, carry):
+            flagged = [masks[2 * lax.div(x, 16) + oy] != 0 for oy in range(2)]
             for c in range(3):
                 for j in range(LANE_TILES):
                     at = pl.multiple_of(c * spread + (x * LANE_TILES + j) * blocks, blocks)
@@ -466,10 +468,10 @@
                     out[c, :, pl.ds(to, 128)] = value.astype(jnp.bfloat16)
             return carry
 
-        lax.fori_loop(0, SPAN, one, 0)
-
-    scatter(ORDER[0])
-    scatter(ORDER[1])
+        lax.fori_loop(*PARTS[part], one, 0)
+
+    scatter(0)
+    scatter(1)
 
     def forward(size):
         for k in others:
@@ -482,7 +484,7 @@
             direct_arrival(k, size).wait_recv()
 
     on_level(0, forward)
-    scatter(ORDER[2])
+    scatter(2)
     on_level(1, gather)
 
     @pl.when(has_fine)
@@ -505,10 +507,10 @@
 
         lax.fori_loop(0, blocks, expand, 0)
 
-    for part in ORDER[:3]:
+    for part in (0, 1, 2):
         finish(part)
-    scatter(ORDER[3])
-    finish(ORDER[3])
+    scatter(3)
+    finish(3)
 
     @pl.when(not_last)
     def _():
@@ -520,7 +522,7 @@
 
     for k in others:
         near(k).wait_send()
-        for part in ORDER:
+        for part in range(len(PARTS)):
             block_copy(part, partners[k]).wait_send()
 
     @pl.when(has_coarse)
@@ -557,8 +559,8 @@
     bf16, f32, i32 = jnp.bfloat16, jnp.float32, jnp.int32
     dma, vm, smem = pltpu.SemaphoreType.DMA, pltpu.VMEM, pltpu.SMEM
     spread = EDGE * LANE_TILES * blocks
-    piece = 3 * SPAN * LANE_TILES
-    parts = EDGE // SPAN
+    pieces = [3 * (x1 - x0) * LANE_TILES for x0, x1 in PARTS]
+    parts = len(PARTS)
     shrink, grow = selection_tables()
     out = pl.pallas_call(
         functools.partial(kernel, n, levels),
@@ -569,9 +571,9 @@
             smem((1, blocks), i32), smem((1, blocks), i32), smem((1, blocks), i32),
             vm((4, blocks, cells), bf16), vm(shrink.shape, bf16), vm(grow.shape, bf16),
             vm((3 * spread, 128), f32), vm((3 * EDGE * (LANE_TILES + 1) * blocks, 128), f32),
-            vm((parts, blocks, piece, 128), bf16), vm((4, blocks, 128), i32),
-            *[vm((n, CAP, piece, 128), bf16)] * parts,
-            *[vm((n * CAP, piece, 128), bf16)] * parts,
+            *[vm((blocks, piece, 128), bf16) for piece in pieces], vm((4, blocks, 128), i32),
+            *[vm((n, CAP, piece, 128), bf16) for piece in pieces],
+            *[vm((n * CAP, piece, 128), bf16) for piece in pieces],
             vm((blocks, 96, 128), bf16), vm((n, CAP, 96, 128), bf16), vm((n * CAP, 96, 128), bf16),
             vm((n * CAP + 1, 96, 128), bf16),
             vm((128, 128), f32), vm((64, 128), bf16), vm((64, 128), bf16),

time: 45.2 us -> 44.6 us (0.987)
  Pallas kernels: 43.8 us -> 43.3 us
    pallas_call x1, Pallas kernels: 43.8 us -> 43.3 us  [body(): pl.pallas_call(functools.partial(kernel, n, levels), out_shape=jax.ShapeD...]
where the time goes in v4:
time: 44.6 us; the launch traced here: 44.4 us
  Pallas kernels  43.3 us (97%)
  local copies, waits for them, and re-layouts  1.15 us (3%)
    pallas_call x1, Pallas kernels, body(): pl.pallas_call(functools.partial(kernel, n, levels), out_shape=jax.ShapeD...  43.3 us
    unnamed x1, local copies, waits for them, and re-layouts  1.15 us

profile of v4, /device:TPU:9, one launch (start us, length us, event | category | flops | bytes accessed | tf_op | source)
XLA Modules:
  0.0 44.4 jit_solution(10913576071671228540)
XLA Ops:
  0.0 43.3 %move.1 = bf16[3,8,32768]{2,1,0:T(8,128)(2,1)S(1)} custom-call(s32[1,8]{1,0:T(1,128)} %spots_in.1, s32[1,8]{1,0:T(1,128)} %parents_in.1, s32[1,8]{1,0:T(1,128)} %flags_in.1, bf16[3,8,32768]{2,1,0:T(8,128)(2,1)} %bitcast.4, bf16[8,32768]{1,0:T(8,128)(2,1)} %bitcast.5, bf16[1024,128]{1,0:T(8,128)(2,1)} %constant.4.clone.shrink_in, ...), custom_call_target="tpu_custom_call" | custom-call | tf_op jit(solution)/shard_map/move/pallas_call | solution.py:565
  43.3 1.1 %copy.9 = bf16[1,3,8,32768]{3,2,1,0:T(8,128)(2,1)} copy(bf16[1,3,8,32768]{3,2,1,0:T(8,128)(2,1)S(1)} %bitcast.3) | data formatting | bytes 3145728

commit v5 on v4

--- a/solution.py
+++ b/solution.py
@@ -13,9 +13,9 @@
 PLANE = EDGE * EDGE
 LANE_TILES = PLANE // 128
 CAP = 2
-PARTS = ((8, 12), (12, 28), (0, 8), (28, 32))
+PARTS = ((4, 8), (8, 20), (20, 32), (0, 4))
 VMEM_LIMIT = 44 * 1024 * 1024
-PIECES = ((6 * PLANE, 14 * PLANE), (14 * PLANE, 32 * PLANE), (0, 6 * PLANE))
+PIECES = ((2 * PLANE, 10 * PLANE), (10 * PLANE, 32 * PLANE), (0, 2 * PLANE))
 
 
 def device(blk, lvl):
@@ -298,8 +298,8 @@
     keep(0)
     remesh(1)
     pack(1)
+    keep(1)
     send_blocks(1)
-    keep(1)
 
     @pl.when(not_last)
     def _():
@@ -369,15 +369,6 @@
 
         lax.fori_loop(0, n, pack_ghost, 0)
 
-    def share(size):
-        for k in others:
-            ghost_copy(k, size).start()
-        relay_copy(0, size).start()
-
-    on_level(0, share)
-    for part in (2, 3):
-        send_blocks(part)
-
     def settle_places(source, places):
         count = jnp.int32(0)
         for b in range(blocks):
@@ -389,8 +380,14 @@
         return places
 
     line[...] = lax.fori_loop(0, n, settle_places, jnp.zeros((1, 128), jnp.int32))
-    fetch_place = pltpu.make_async_copy(line, place, table_sem.at[3])
-    fetch_place.start()
+    def share(size):
+        for k in others:
+            ghost_copy(k, size).start()
+        relay_copy(0, size).start()
+
+    on_level(0, share)
+    for part in (2, 3):
+        send_blocks(part)
 
     @pl.when(has_fine)
     def _():
@@ -425,9 +422,11 @@
 
     rounds = jnp.where(has_fine, n, 0)
     line2[...] = lax.fori_loop(0, rounds, settle_octants, jnp.full((1, 128), empty, jnp.int32))
+    got_ghost[empty] = jnp.zeros(got_ghost.shape[1:], jnp.bfloat16)
+    fetch_place = pltpu.make_async_copy(line, place, table_sem.at[3])
     fetch_octants = pltpu.make_async_copy(line2, octants, table_sem.at[5])
+    fetch_place.start()
     fetch_octants.start()
-    got_ghost[empty] = jnp.zeros(got_ghost.shape[1:], jnp.bfloat16)
     fetch_place.wait()
     fetch_octants.wait()
 

time: 44.6 us -> 44.8 us (level)
  no operation moved by 1% of the time
where the time goes in v5:
time: 44.8 us; the launch traced here: 44.4 us
  Pallas kernels  43.3 us (97%)
  local copies, waits for them, and re-layouts  1.15 us (3%)
    pallas_call x1, Pallas kernels, body(): pl.pallas_call(functools.partial(kernel, n, levels), out_shape=jax.ShapeD...  43.3 us
    unnamed x1, local copies, waits for them, and re-layouts  1.15 us

profile of v5, /device:TPU:9, one launch (start us, length us, event | category | flops | bytes accessed | tf_op | source)
XLA Modules:
  0.0 44.4 jit_solution(16919654619422370670)
XLA Ops:
  0.0 43.3 %move.1 = bf16[3,8,32768]{2,1,0:T(8,128)(2,1)S(1)} custom-call(s32[1,8]{1,0:T(1,128)} %spots_in.1, s32[1,8]{1,0:T(1,128)} %parents_in.1, s32[1,8]{1,0:T(1,128)} %flags_in.1, bf16[3,8,32768]{2,1,0:T(8,128)(2,1)} %bitcast.4, bf16[8,32768]{1,0:T(8,128)(2,1)} %bitcast.5, bf16[1024,128]{1,0:T(8,128)(2,1)} %constant.4.clone.shrink_in, ...), custom_call_target="tpu_custom_call" | custom-call | tf_op jit(solution)/shard_map/move/pallas_call | solution.py:564
  43.3 1.1 %copy.9 = bf16[1,3,8,32768]{3,2,1,0:T(8,128)(2,1)} copy(bf16[1,3,8,32768]{3,2,1,0:T(8,128)(2,1)S(1)} %bitcast.3) | data formatting | bytes 3145728

commit v6 on v5

--- a/solution.py
+++ b/solution.py
@@ -13,7 +13,7 @@
 PLANE = EDGE * EDGE
 LANE_TILES = PLANE // 128
 CAP = 2
-PARTS = ((4, 8), (8, 20), (20, 32), (0, 4))
+PARTS = ((4, 8), (8, 22), (22, 32), (0, 4))
 VMEM_LIMIT = 44 * 1024 * 1024
 PIECES = ((2 * PLANE, 10 * PLANE), (10 * PLANE, 32 * PLANE), (0, 2 * PLANE))
 

time: 44.8 us -> 44.8 us (level)
  no operation moved by 1% of the time
where the time goes in v6:
time: 44.8 us; the launch traced here: 44.4 us
  Pallas kernels  43.3 us (97%)
  local copies, waits for them, and re-layouts  1.15 us (3%)
    pallas_call x1, Pallas kernels, body(): pl.pallas_call(functools.partial(kernel, n, levels), out_shape=jax.ShapeD...  43.3 us
    unnamed x1, local copies, waits for them, and re-layouts  1.15 us

profile of v6, /device:TPU:9, one launch (start us, length us, event | category | flops | bytes accessed | tf_op | source)
XLA Modules:
  0.0 44.4 jit_solution(17569518837905952838)
XLA Ops:
  0.0 43.3 %move.1 = bf16[3,8,32768]{2,1,0:T(8,128)(2,1)S(1)} custom-call(s32[1,8]{1,0:T(1,128)} %spots_in.1, s32[1,8]{1,0:T(1,128)} %parents_in.1, s32[1,8]{1,0:T(1,128)} %flags_in.1, bf16[3,8,32768]{2,1,0:T(8,128)(2,1)} %bitcast.4, bf16[8,32768]{1,0:T(8,128)(2,1)} %bitcast.5, bf16[1024,128]{1,0:T(8,128)(2,1)} %constant.4.clone.shrink_in, ...), custom_call_target="tpu_custom_call" | custom-call | tf_op jit(solution)/shard_map/move/pallas_call | solution.py:564
  43.3 1.1 %copy.9 = bf16[1,3,8,32768]{3,2,1,0:T(8,128)(2,1)} copy(bf16[1,3,8,32768]{3,2,1,0:T(8,128)(2,1)S(1)} %bitcast.3) | data formatting | bytes 3145728

commit v7 on v6

--- a/solution.py
+++ b/solution.py
@@ -508,9 +508,6 @@
 
     for part in (0, 1, 2):
         finish(part)
-    scatter(3)
-    finish(3)
-
     @pl.when(not_last)
     def _():
         high(after).wait_send()
@@ -521,7 +518,7 @@
 
     for k in others:
         near(k).wait_send()
-        for part in range(len(PARTS)):
+        for part in (0, 1, 2):
             block_copy(part, partners[k]).wait_send()
 
     @pl.when(has_coarse)
@@ -536,6 +533,12 @@
             direct_copy(k, size).wait_send()
 
     on_level(0, drain)
+
+    scatter(3)
+    finish(3)
+
+    for k in others:
+        block_copy(3, partners[k]).wait_send()
 
 
 def selection_tables():

time: 44.8 us -> 44.6 us (level)
  no operation moved by 1% of the time
where the time goes in v7:
time: 44.6 us; the launch traced here: 44.3 us
  Pallas kernels  43.2 us (97%)
  local copies, waits for them, and re-layouts  1.15 us (3%)
    pallas_call x1, Pallas kernels, body(): pl.pallas_call(functools.partial(kernel, n, levels), out_shape=jax.ShapeD...  43.2 us
    unnamed x1, local copies, waits for them, and re-layouts  1.15 us

profile of v7, /device:TPU:9, one launch (start us, length us, event | category | flops | bytes accessed | tf_op | source)
XLA Modules:
  0.0 44.3 jit_solution(383868759180016167)
XLA Ops:
  0.0 43.2 %move.1 = bf16[3,8,32768]{2,1,0:T(8,128)(2,1)S(1)} custom-call(s32[1,8]{1,0:T(1,128)} %spots_in.1, s32[1,8]{1,0:T(1,128)} %parents_in.1, s32[1,8]{1,0:T(1,128)} %flags_in.1, bf16[3,8,32768]{2,1,0:T(8,128)(2,1)} %bitcast.4, bf16[8,32768]{1,0:T(8,128)(2,1)} %bitcast.5, bf16[1024,128]{1,0:T(8,128)(2,1)} %constant.4.clone.shrink_in, ...), custom_call_target="tpu_custom_call" | custom-call | tf_op jit(solution)/shard_map/move/pallas_call | solution.py:567
  43.2 1.1 %copy.9 = bf16[1,3,8,32768]{3,2,1,0:T(8,128)(2,1)} copy(bf16[1,3,8,32768]{3,2,1,0:T(8,128)(2,1)S(1)} %bitcast.3) | data formatting | bytes 3145728
